TPU v7x, 512 devices: a whole 4x8x8 slice. The times are simulated.
512 devices in a mesh: elem: 32 (over z, x), lev: 16 (over y, core).
Axes of the slice: x: 4, y: 8, z: 8, core: 2. Of those that a mesh axis runs over, the one named last changes fastest.
Arguments:
- cloud_state: float32 [4096, 8, 4096], P(('elem', 'lev')), may hold values from -6 to 6
- substeps: int32 [4096], P('elem'), may hold values from 4 to 16
- element_links: int32 [1024, 4], P('elem'), may hold values from 0 to 1023, as said below
- host_state: float32 [4, 64, 16384], P(None, 'lev', 'elem'), may hold values from -6 to 6
- wind_field: float32 [2, 64, 16384], P(None, 'lev', 'elem'), may hold values from -3 to 3
- node_mass: float32 [16384], P('elem'), may hold values from 0.25 to 4
- field_coupling: float32 [8, 8], replicated, may hold values from -2 to 2
- force_map: float32 [8, 4], replicated, may hold values from -3 to 3
- feedback_map: float32 [4, 8], replicated, may hold values from -5 to 5
Outputs:
- cloud_new: float32 [4096, 8, 4096], P(('elem', 'lev'))
- host_new: float32 [4, 64, 16384], P(None, 'lev', 'elem')
Inputs may be any that keep to these rules, and one draw needn't show every extreme that they name: `element_links`: the 1024 elements form a doubly periodic grid of 16 rows in which each index of elem holds two neighbouring grid columns, all rows, in some order; element e lies on index e // 32 of elem. Entries 0 to 3 of row e give the global index of the element to the left, right, below and above element e. An element's right edge meets its right neighbour's left edge node for node (same j), its upper edge its upper neighbour's lower edge (same i). The left neighbour lies on the same index of elem or the one before it (cyclically), the right one on the same or the one after it, the lower and upper ones on the same index.
All inputs are finite; a program needn't handle non-finite values.
Results may differ from a plain program's by a relative error of at most 0.0003.
Values sent between devices are 32-bit elements; how exact they have to be, the bound alone decides.
No kernel may reach another device: no remote copies, remote signals or barrier semaphores. Data moves between devices by JAX's collectives and lax.ppermute only.
A program may use at most 64 MiB of HBM per device.

v0:
```python
import jax
import jax.numpy as jnp
import numpy as np
from jax import lax
from jax.sharding import PartitionSpec as P

CRM_X = 64
lateral_mix = 0.2
vertical_mix = 0.2
cloud_step = 0.1
host_step = 0.1
host_mix = 0.2
highest = lax.Precision.HIGHEST


def padded_2(cells, sides, width, closed):
    for axis, dim in sides:
        count = lax.axis_size(axis)
        ends = count if closed else count - 1
        head = lax.slice_in_dim(cells, 0, width, axis=dim)
        tail = lax.slice_in_dim(cells, cells.shape[dim] - width, cells.shape[dim], axis=dim)
        cells = jnp.concatenate(
            [
                lax.ppermute(tail, axis, [(i, (i + 1) % count) for i in range(ends)]),
                cells,
                lax.ppermute(head, axis, [((i + 1) % count, i) for i in range(ends)]),
            ],
            axis=dim,
        )
    return cells


def gll_derivative():
    points = np.array([-1.0, -1.0 / np.sqrt(5.0), 1.0 / np.sqrt(5.0), 1.0])
    weights = np.array(
        [
            1.0 / np.prod([points[index] - points[other] for other in range(4) if other != index])
            for index in range(4)
        ]
    )
    matrix = np.zeros((4, 4))
    for target in range(4):
        for source in range(4):
            if target != source:
                matrix[target, source] = (
                    weights[source] / weights[target] / (points[target] - points[source])
                )
        matrix[target, target] = -np.sum(matrix[target])
    return matrix


def advance_clouds(cloud, driving, counts, coupling):
    n_rows, n_fields, n_cells = cloud.shape
    cell_width = CRM_X
    n_levels = n_cells // cell_width
    spread = jnp.repeat(driving, cell_width, axis=2)

    def one_step(stepno, current):
        extended = jnp.pad(current, ((0, 0), (0, 0), (cell_width, cell_width)))
        upper_cells = extended[:, :, 2 * cell_width :]
        lower_cells = extended[:, :, : -2 * cell_width]
        shaped = current.reshape(n_rows, n_fields, n_levels, cell_width)
        eastward = jnp.roll(shaped, -1, axis=3).reshape(current.shape)
        westward = jnp.roll(shaped, 1, axis=3).reshape(current.shape)
        reaction = jnp.tanh(jnp.einsum("gf,nfc->ngc", coupling, current, precision=highest))
        update = (
            current
            + (
                lateral_mix * (eastward + westward - 2.0 * current)
                + vertical_mix * (upper_cells + lower_cells - 2.0 * current)
            )
            + cloud_step * (reaction + spread)
        )
        return jnp.where((stepno < counts)[:, None, None], update, current)

    return lax.fori_loop(0, jnp.max(counts), one_step, cloud)


def edge_tables(element_links, n_nodes):
    elem_dev = n_nodes // 16
    quarter = 4 * elem_dev
    my_index = lax.axis_index("elem")
    node_ids = jnp.arange(n_nodes, dtype=jnp.int32)
    elem_of = node_ids // 16
    row_of = node_ids // 4 % 4
    col_of = node_ids % 4
    edge_ids = jnp.arange(2 * quarter, dtype=jnp.int32)
    inner = edge_ids % quarter
    edge_node = inner // 4 * 16 + inner % 4 * 4 + jnp.where(edge_ids < quarter, 0, 3)
    picker = (node_ids[:, None] == edge_node[None, :]).astype(jnp.float32)
    left_ids = element_links[:, 0][elem_of]
    right_ids = element_links[:, 1][elem_of]
    left_base = jnp.where(left_ids // elem_dev == my_index, 2 * quarter, 0)
    right_base = jnp.where(right_ids // elem_dev == my_index, 2 * quarter, 4 * quarter)
    left_source = left_base + quarter + left_ids % elem_dev * 4 + row_of
    right_source = right_base + right_ids % elem_dev * 4 + row_of
    side_source = jnp.where(col_of == 0, left_source, jnp.where(col_of == 3, right_source, -1))
    sideways = (jnp.arange(6 * quarter, dtype=jnp.int32)[:, None] == side_source[None, :]).astype(
        jnp.float32
    )
    lower_ids = element_links[:, 2][elem_of] % elem_dev
    upper_ids = element_links[:, 3][elem_of] % elem_dev
    lower_source = lower_ids * 16 + 12 + col_of
    upper_source = upper_ids * 16 + col_of
    vert_source = jnp.where(row_of == 0, lower_source, jnp.where(row_of == 3, upper_source, -1))
    vertical = (node_ids[:, None] == vert_source[None, :]).astype(jnp.float32)
    return (picker, sideways, vertical)


def edge_sum(quantity, tables):
    picker, sideways, vertical = tables
    lead, levels, n_nodes = quantity.shape
    flat = quantity.reshape(lead * levels, n_nodes)
    edges = jnp.dot(flat, picker, precision=highest).reshape(lead, levels, picker.shape[1])
    with_peers = padded_2(edges, (("elem", 2),), picker.shape[1], True)
    first = flat + jnp.dot(
        with_peers.reshape(lead * levels, sideways.shape[0]), sideways, precision=highest
    )
    second = first + jnp.dot(first, vertical, precision=highest)
    return second.reshape(lead, levels, n_nodes)


def shards(
    cloud_state,
    substeps,
    element_links,
    host_state,
    wind_field,
    node_mass,
    field_coupling,
    force_map,
    feedback_map,
):
    own_rows, n_fields, n_cells = cloud_state.shape
    n_vars, lev_dev, n_nodes = host_state.shape
    n_cols = substeps.shape[0]
    elem_dev = n_nodes // 16
    cell_width = CRM_X
    lev_at = lax.axis_index("lev")
    node_ids = jnp.arange(n_nodes)
    column_of_node = node_ids // 16 * 4 + node_ids // 4 % 4 // 2 * 2 + node_ids % 4 // 2
    member = (column_of_node[:, None] == jnp.arange(n_cols)[None, :]).astype(jnp.float32)
    pooling = 0.25 * member
    host_flat = host_state.reshape(n_vars * lev_dev, n_nodes)
    host_columns = (
        jnp.dot(host_flat, pooling, precision=highest)
        .reshape(n_vars, lev_dev, n_cols)
        .transpose(2, 0, 1)
    )
    every_host = lax.all_gather(host_columns, "lev", axis=2, tiled=True)
    whole_host = lax.dynamic_slice_in_dim(every_host, lev_at * own_rows, own_rows, 0)
    driving = jnp.einsum("fv,nvl->nfl", force_map, whole_host, precision=highest)
    own_counts = lax.dynamic_slice_in_dim(substeps, lev_at * own_rows, own_rows, 0)
    cloud_new = advance_clouds(cloud_state, driving, own_counts, field_coupling)
    n_levels = n_cells // cell_width
    change = (
        (cloud_new - cloud_state).reshape(own_rows, n_fields, n_levels, cell_width).mean(axis=3)
    )
    every_change = lax.all_gather(change, "lev", axis=0, tiled=True)
    level_change = lax.dynamic_slice_in_dim(every_change, lev_at * lev_dev, lev_dev, 2)
    column_tendency = jnp.einsum("vf,nfl->vln", feedback_map, level_change, precision=highest)
    physics = jnp.dot(
        column_tendency.reshape(n_vars * lev_dev, n_cols), member.T, precision=highest
    ).reshape(n_vars, lev_dev, n_nodes)
    derivative = gll_derivative()
    kron_x = jnp.asarray(np.kron(np.eye(elem_dev * 4), derivative).T, jnp.float32)
    kron_y = jnp.asarray(np.kron(np.eye(elem_dev), np.kron(derivative, np.eye(4))).T, jnp.float32)

    def tendency(field):
        flat = field.reshape(n_vars * lev_dev, n_nodes)
        along_x = jnp.dot(flat, kron_x, precision=highest).reshape(field.shape)
        along_y = jnp.dot(flat, kron_y, precision=highest).reshape(field.shape)
        padded = padded_2(field, (("lev", 1),), 1, False)
        return (
            -(wind_field[0] * along_x + wind_field[1] * along_y)
            + host_mix * (padded[:, 2:] + padded[:, :-2] - 2.0 * field)
            + physics
        )

    tables = edge_tables(element_links, n_nodes)
    mass_total = edge_sum(node_mass.reshape(1, 1, n_nodes), tables)

    def smooth(values):
        return edge_sum(node_mass * values, tables) / mass_total

    first_section = smooth(host_state + host_step * tendency(host_state))
    second_section = smooth(
        0.75 * host_state + 0.25 * (first_section + host_step * tendency(first_section))
    )
    host_new = smooth(
        host_state / 3.0 + 2.0 / 3.0 * (second_section + host_step * tendency(second_section))
    )
    return (cloud_new, host_new)


def solution(mesh):
    placed = (
        P(("elem", "lev"), None, None),
        P("elem"),
        P("elem", None),
        P(None, "lev", "elem"),
        P(None, "lev", "elem"),
        P("elem"),
        P(),
        P(),
        P(),
    )
    return jax.shard_map(
        shards,
        mesh=mesh,
        in_specs=placed,
        out_specs=(P(("elem", "lev"), None, None), P(None, "lev", "elem")),
        check_vma=False,
    )
```

profile of v0, /device:TPU:230, one launch (start us, length us, event | category | flops | bytes accessed | tf_op | source)
XLA Modules:
  0.0 390.2 jit_solution(18212692638045972472)
XLA Ops:
  0.7 1.0 convolution_bitcast_fusion.4
  1.7 5.4 %collective-permute-start.4 = (f32[1,1,256]{2,1,0:T(1,128)S(1)}, f32[1,1,256]{2,1,0:T(1,128)S(1)}, u32[]{:S(2)}, u32[]{:S(2)}) collective-permute-start(f32[1,1,256]{2,1,0:T(1,128)S(1)} %convolution_bitcast_fusion.4), channel_id=1, source_target_pairs={{0,16},{16,32},{32,48},{48,64},{64,80},{80,96},{96,112},{112,128},... | collective-permute-start | bytes 3080 | tf_op jit(solution)/shard_map/ppermute | solution.py:24
  7.1 1.9 collective-permute-start.5
  9.9 1.9 collective-permute-start
  11.8 2.4 collective-permute-start.1
  14.3 2.1 fusion.138
  16.4 2.1 fusion.137
  18.4 2.1 fusion.136
  20.6 1.9 fusion.139
  24.1 2.1 fusion.134
  26.2 2.1 fusion.133
  28.3 2.1 fusion.135
  30.8 15.3 %all_gather.6 = f32[128,4,64]{0,1,2:T(4,128)S(1)} all-gather(f32[128,4,4]{0,1,2:T(4,128)S(1)} %bitcast.238), channel_id=1, replica_groups=mesh['elem'=32,'lev'=16] {'lev'}, dimensions={2}, use_global_device_ids=true | all-gather | bytes 139264 | tf_op jit(solution)/shard_map/all_gather | solution.py:150
  46.3 1.5 fusion.127
  48.0 68.8 %while.13 = (s32[]{:T(128)}, f32[8,8,4096]{2,1,0:T(8,128)S(1)}, s32[]{:T(128)}, s32[8]{0:T(128)S(1)}, f32[8,8]{1,0:T(8,128)S(1)}, /*index=5*/f32[8,8,64]{2,1,0:T(8,128)S(1)}, s32[]{:T(128)}) while((s32[]{:T(128)}, f32[8,8,4096]{2,1,0:T(8,128)S(1)}, s32[]{:T(128)}, s32[8]{0:T(128)S(1)}, f32[8,8]{1,0:T(8,128)S(1)}, ...), condition=%wide.region_2.3_spmd.clone, body=%wide.region_1.2_spmd.clone.sunk | while | flops 28835848 | bytes 22041208 | solution.py:76
  51.1 1.2 maximum_add_fusion.2
  52.3 1.6 add.880
  54.5 1.6 reshape.997
  56.1 3.2 fusion.176
  62.5 1.2 maximum_add_fusion.2
  63.6 1.6 add.880
  65.9 1.6 reshape.997
  67.5 3.2 fusion.176
  73.8 1.2 maximum_add_fusion.2
  75.0 1.6 add.880
  77.2 1.6 reshape.997
  78.8 3.2 fusion.176
  85.1 1.2 maximum_add_fusion.2
  86.3 1.6 add.880
  88.6 1.6 reshape.997
  90.2 3.2 fusion.176
  96.5 1.2 maximum_add_fusion.2
  97.6 1.6 add.880
  99.9 1.6 reshape.997
  101.5 3.2 fusion.176
  107.8 1.2 maximum_add_fusion.2
  109.0 1.6 add.880
  111.2 1.6 reshape.997
  112.9 3.2 fusion.176
  116.8 1.8 sub.95
  118.6 2.2 reshape.403
  120.8 2.3 reduce_sum.9
  123.1 17.1 %all_gather.7 = f32[128,8,64]{2,1,0:T(8,128)S(1)} all-gather(f32[8,8,64]{2,1,0:T(8,128)S(1)} %broadcast_multiply_fusion), channel_id=1, replica_groups=mesh['elem'=32,'lev'=16] {'lev'}, dimensions={0}, use_global_device_ids=true | all-gather | bytes 278528 | tf_op jit(solution)/shard_map/all_gather | solution.py:159
  141.9 4.2 %select_select_fusion.3 = s32[512,1]{0,1:T(1,128)S(1)} fusion(s32[]{:T(128)} %bitcast.40, s32[]{:T(128)} %bitcast.41, s32[]{:T(128)} %bitcast.42, s32[]{:T(128)} %bitcast.43, s32[]{:T(128)} %bitcast.44, s32[]{:T(128)} %bitcast.46, s32[]{:T(128)} %bitcast.45), kind=kLoop, calls=%fused_computation.216 | loop fusion | flops 11776 | bytes 2076 | tf_op jit(solution)/shard_map/gather | solution.py:91
  146.1 4.4 %select_select_fusion.2 = s32[512,1]{0,1:T(1,128)S(1)} fusion(s32[]{:T(128)} %bitcast.73, s32[]{:T(128)} %bitcast.74, s32[]{:T(128)} %bitcast.75, s32[]{:T(128)} %bitcast.76, s32[]{:T(128)} %bitcast.77, s32[]{:T(128)} %bitcast.79, s32[]{:T(128)} %bitcast.78), kind=kLoop, calls=%fused_computation.215 | loop fusion | flops 11776 | bytes 2076 | tf_op jit(solution)/shard_map/gather | solution.py:92
  150.4 4.4 %select_select_fusion.1 = s32[512,1]{0,1:T(1,128)S(1)} fusion(s32[]{:T(128)} %bitcast.106, s32[]{:T(128)} %bitcast.107, s32[]{:T(128)} %bitcast.108, s32[]{:T(128)} %bitcast.109, s32[]{:T(128)} %bitcast.110, s32[]{:T(128)} %bitcast.112, s32[]{:T(128)} %bitcast.111), kind=kLoop, calls=%fused_computation.214 | loop fusion | flops 11776 | bytes 2076 | tf_op jit(solution)/shard_map/gather | solution.py:101
  154.9 4.5 %select_select_fusion = s32[512,1]{0,1:T(1,128)S(1)} fusion(s32[]{:T(128)} %bitcast.139, s32[]{:T(128)} %bitcast.140, s32[]{:T(128)} %bitcast.141, s32[]{:T(128)} %bitcast.142, s32[]{:T(128)} %bitcast.143, s32[]{:T(128)} %bitcast.145, s32[]{:T(128)} %bitcast.144), kind=kLoop, calls=%fused_computation.213 | loop fusion | flops 11776 | bytes 2076 | tf_op jit(solution)/shard_map/gather | solution.py:102
  159.3 30.8 %fusion.104 = s32[512]{0:T(512)S(1)} fusion(pred[512]{0:T(512)(128)(4,1)S(1)} %compare_reduce_fusion, pred[512]{0:T(512)(128)(4,1)S(1)} %compare_reduce_fusion.1, pred[512]{0:T(512)(128)(4,1)S(1)} %compare_reduce_fusion.2, pred[512]{0:T(512)(128)(4,1)S(1)} %compare_reduce_fusion.3, pred[512]{0:T(512)(128)(4,1)S(1)} %compare_reduce_fusion.4, ...), kind=kLoop, calls=%fused_computation.204 | loop fusion | flops 53248 | bytes 19144 | tf_op jit(solution)/shard_map/jit(_where)/select_n | solution.py:105
  190.2 31.2 %fusion.94 = s32[512]{0:T(512)S(1)} fusion(pred[512]{0:T(512)(128)(4,1)S(1)} %compare_reduce_fusion, pred[512]{0:T(512)(128)(4,1)S(1)} %compare_reduce_fusion.1, pred[512]{0:T(512)(128)(4,1)S(1)} %compare_reduce_fusion.2, pred[512]{0:T(512)(128)(4,1)S(1)} %compare_reduce_fusion.3, pred[512]{0:T(512)(128)(4,1)S(1)} %compare_reduce_fusion.4, ...), kind=kLoop, calls=%fused_computation.194 | loop fusion | flops 64512 | bytes 19148 | tf_op jit(solution)/shard_map/jit(_where)/select_n | solution.py:97
  223.1 7.2 %collective-permute-start.2 = (f32[4,4,256]{2,1,0:T(4,128)S(1)}, f32[4,4,256]{2,1,0:T(4,128)S(1)}, u32[]{:S(2)}, u32[]{:S(2)}) collective-permute-start(f32[4,4,256]{2,1,0:T(4,128)S(1)} %fusion.37), channel_id=1, source_target_pairs={{0,16},{16,32},{32,48},{48,64},{64,80},{80,96},{96,112},{112,128},... | collective-permute-start | bytes 49160 | tf_op jit(solution)/shard_map/ppermute | solution.py:24
  230.3 1.9 collective-permute-start.3
  232.7 6.6 %collective-permute-done.3 = f32[4,4,256]{2,1,0:T(4,128)S(1)} collective-permute-done((f32[4,4,256]{2,1,0:T(4,128)S(1)}, f32[4,4,256]{2,1,0:T(4,128)S(1)}, u32[]{:S(2)}, u32[]{:S(2)}) %collective-permute-start.3) | collective-permute-done | bytes 16416 | tf_op jit(solution)/shard_map/ppermute | solution.py:26
  240.4 1.9 collective-permute-start.6
  242.3 2.4 collective-permute-start.7
  245.4 3.1 collective-permute-done.7
  249.5 1.9 collective-permute-start.8
  251.4 104.3 %collective-permute-start.9 = (f32[4,4,256]{2,1,0:T(4,128)S(1)}, f32[4,4,256]{2,1,0:T(4,128)S(1)}, u32[]{:S(2)}, u32[]{:S(2)}) collective-permute-start(f32[4,4,256]{2,1,0:T(4,128)S(1)} %fusion.35), channel_id=1, source_target_pairs={{16,0},{32,16},{48,32},{64,48},{80,64},{96,80},{112,96},{128,112},... | collective-permute-start | bytes 49160 | tf_op jit(solution)/shard_map/ppermute | solution.py:26
  355.7 1.4 collective-permute-done.9
  358.2 1.9 collective-permute-start.10
  360.1 2.4 collective-permute-start.11
  363.2 3.1 collective-permute-done.11
  367.3 12.3 %collective-permute-start.12 = (f32[4,4,256]{2,1,0:T(4,128)S(1)}, f32[4,4,256]{2,1,0:T(4,128)S(1)}, u32[]{:S(2)}, u32[]{:S(2)}) collective-permute-start(f32[4,4,256]{2,1,0:T(4,128)S(1)} %fusion.33), channel_id=1, source_target_pairs={{0,16},{16,32},{32,48},{48,64},{64,80},{80,96},{96,112},{112,128},... | collective-permute-start | bytes 49160 | tf_op jit(solution)/shard_map/ppermute | solution.py:24
  379.5 1.9 collective-permute-start.13
  381.5 7.0 %collective-permute-done.13 = f32[4,4,256]{2,1,0:T(4,128)S(1)} collective-permute-done((f32[4,4,256]{2,1,0:T(4,128)S(1)}, f32[4,4,256]{2,1,0:T(4,128)S(1)}, u32[]{:S(2)}, u32[]{:S(2)}) %collective-permute-start.13) | collective-permute-done | bytes 16416 | tf_op jit(solution)/shard_map/ppermute | solution.py:26
  (143 shorter events, 32.0 us)
Async XLA Ops:
  0.6 47.1 %copy-start = (f32[8,4]{0,1:T(4,128)S(1)}, f32[8,4]{0,1:T(4,128)}, u32[]{:S(2)}) copy-start(f32[8,4]{0,1:T(4,128)} %param.20) | copy-start | bytes 388
  0.6 47.3 %copy-start.2 = (f32[8,8,4096]{2,1,0:T(8,128)S(1)}, f32[8,8,4096]{2,1,0:T(8,128)}, u32[]{:S(2)}) copy-start(f32[8,8,4096]{2,1,0:T(8,128)} %param.13) | copy-start | bytes 3145732
  0.7 47.3 %copy-start.6 = (f32[8,8]{1,0:T(8,128)S(1)}, f32[8,8]{1,0:T(8,128)}, u32[]{:S(2)}) copy-start(f32[8,8]{1,0:T(8,128)} %param.19) | copy-start | bytes 772
  1.7 219.8 %collective-permute-start.4 = (f32[1,1,256]{2,1,0:T(1,128)S(1)}, f32[1,1,256]{2,1,0:T(1,128)S(1)}, u32[]{:S(2)}, u32[]{:S(2)}) collective-permute-start(f32[1,1,256]{2,1,0:T(1,128)S(1)} %convolution_bitcast_fusion.4), channel_id=1, source_target_pairs={{0,16},{16,32},{32,48},{48,64},{64,80},{80,96},{96,112},{112,128},... | collective-permute-start | bytes 3080 | tf_op jit(solution)/shard_map/ppermute | solution.py:24
  7.1 214.3 %collective-permute-start.5 = (f32[1,1,256]{2,1,0:T(1,128)S(1)}, f32[1,1,256]{2,1,0:T(1,128)S(1)}, u32[]{:S(2)}, u32[]{:S(2)}) collective-permute-start(f32[1,1,256]{2,1,0:T(1,128)S(1)} %convolution_bitcast_fusion.4), channel_id=1, source_target_pairs={{16,0},{32,16},{48,32},{64,48},{80,64},{96,80},{112,96},{128,112},... | collective-permute-start | bytes 3080 | tf_op jit(solution)/shard_map/ppermute | solution.py:26
  9.9 212.1 %collective-permute-start = (f32[4,1,512]{2,1,0:T(1,128)S(1)}, f32[4,1,512]{2,1,0:T(1,128)S(1)}, u32[]{:S(2)}, u32[]{:S(2)}) collective-permute-start(f32[4,1,512]{2,1,0:T(1,128)S(1)} %get-tuple-element.121), channel_id=1, source_target_pairs={{1,0},{2,1},{3,2},{4,3},{5,4},{6,5},{7,6},{8,7},{9,8},{10,9},{11,1... | collective-permute-start | bytes 24584 | tf_op jit(solution)/shard_map/ppermute | solution.py:26
  11.8 210.2 %collective-permute-start.1 = (f32[4,1,512]{2,1,0:T(1,128)S(1)}, f32[4,1,512]{2,1,0:T(1,128)S(1)}, u32[]{:S(2)}, u32[]{:S(2)}) collective-permute-start(f32[4,1,512]{2,1,0:T(1,128)S(1)} %get-tuple-element.122), channel_id=1, source_target_pairs={{0,1},{1,2},{2,3},{3,4},{4,5},{5,6},{6,7},{7,8},{8,9},{9,10},{10,1... | collective-permute-start | bytes 24584 | tf_op jit(solution)/shard_map/ppermute | solution.py:24
  116.7 4.0 %copy-start.1 = (f32[8,8,4096]{2,1,0:T(8,128)}, f32[8,8,4096]{2,1,0:T(8,128)S(1)}, u32[]{:S(2)}) copy-start(f32[8,8,4096]{2,1,0:T(8,128)S(1)} %get-tuple-element.80) | copy-start | bytes 3145732
  120.7 19.9 %copy-start.9 = (f32[4,8]{1,0:T(4,128)S(1)}, f32[4,8]{1,0:T(4,128)}, u32[]{:S(2)}) copy-start(f32[4,8]{1,0:T(4,128)} %param.21) | copy-start | bytes 388
  120.7 20.4 %copy-start.8 = (f32[2,4,512]{2,1,0:T(4,128)S(1)}, f32[2,4,512]{2,1,0:T(4,128)}, u32[]{:S(2)}) copy-start(f32[2,4,512]{2,1,0:T(4,128)} %param.17) | copy-start | bytes 49156
  120.7 20.4 %copy-start.4 = (f32[512,512,1]{1,0,2:T(8,128)S(1)}, f32[512,512,1]{1,0,2:T(8,128)}, u32[]{:S(2)}) copy-start(f32[512,512,1]{1,0,2:T(8,128)} %constant.378) | copy-start | bytes 3145732
  120.8 20.4 %copy-start.5 = (f32[4,4,512]{2,1,0:T(4,128)S(1)}, f32[4,4,512]{2,1,0:T(4,128)}, u32[]{:S(2)}) copy-start(f32[4,4,512]{2,1,0:T(4,128)} %param.16) | copy-start | bytes 98308
  123.1 98.9 %copy-start.7 = (f32[512]{0:T(512)S(1)}, f32[512]{0:T(512)}, u32[]{:S(2)}) copy-start(f32[512]{0:T(512)} %param.18) | copy-start | bytes 6148
  123.1 99.0 %copy-start.3 = (f32[512,512,1]{1,0,2:T(8,128)S(1)}, f32[512,512,1]{1,0,2:T(8,128)}, u32[]{:S(2)}) copy-start(f32[512,512,1]{1,0,2:T(8,128)} %constant.379) | copy-start | bytes 3145732
  223.1 9.6 %collective-permute-start.2 = (f32[4,4,256]{2,1,0:T(4,128)S(1)}, f32[4,4,256]{2,1,0:T(4,128)S(1)}, u32[]{:S(2)}, u32[]{:S(2)}) collective-permute-start(f32[4,4,256]{2,1,0:T(4,128)S(1)} %fusion.37), channel_id=1, source_target_pairs={{0,16},{16,32},{32,48},{48,64},{64,80},{80,96},{96,112},{112,128},... | collective-permute-start | bytes 49160 | tf_op jit(solution)/shard_map/ppermute | solution.py:24
  230.3 9.0 %collective-permute-start.3 = (f32[4,4,256]{2,1,0:T(4,128)S(1)}, f32[4,4,256]{2,1,0:T(4,128)S(1)}, u32[]{:S(2)}, u32[]{:S(2)}) collective-permute-start(f32[4,4,256]{2,1,0:T(4,128)S(1)} %fusion.37), channel_id=1, source_target_pairs={{16,0},{32,16},{48,32},{64,48},{80,64},{96,80},{112,96},{128,112},... | collective-permute-start | bytes 49160 | tf_op jit(solution)/shard_map/ppermute | solution.py:26
  240.4 5.0 %collective-permute-start.6 = (f32[4,1,512]{2,1,0:T(1,128)S(1)}, f32[4,1,512]{2,1,0:T(1,128)S(1)}, u32[]{:S(2)}, u32[]{:S(2)}) collective-permute-start(f32[4,1,512]{2,1,0:T(1,128)S(1)} %get-tuple-element.119), channel_id=1, source_target_pairs={{1,0},{2,1},{3,2},{4,3},{5,4},{6,5},{7,6},{8,7},{9,8},{10,9},{11,1... | collective-permute-start | bytes 24584 | tf_op jit(solution)/shard_map/ppermute | solution.py:26
  242.3 6.2 %collective-permute-start.7 = (f32[4,1,512]{2,1,0:T(1,128)S(1)}, f32[4,1,512]{2,1,0:T(1,128)S(1)}, u32[]{:S(2)}, u32[]{:S(2)}) collective-permute-start(f32[4,1,512]{2,1,0:T(1,128)S(1)} %get-tuple-element.120), channel_id=1, source_target_pairs={{0,1},{1,2},{2,3},{3,4},{4,5},{5,6},{6,7},{7,8},{8,9},{9,10},{10,1... | collective-permute-start | bytes 24584 | tf_op jit(solution)/shard_map/ppermute | solution.py:24
  249.5 106.2 %collective-permute-start.8 = (f32[4,4,256]{2,1,0:T(4,128)S(1)}, f32[4,4,256]{2,1,0:T(4,128)S(1)}, u32[]{:S(2)}, u32[]{:S(2)}) collective-permute-start(f32[4,4,256]{2,1,0:T(4,128)S(1)} %fusion.35), channel_id=1, source_target_pairs={{0,16},{16,32},{32,48},{48,64},{64,80},{80,96},{96,112},{112,128},... | collective-permute-start | bytes 49160 | tf_op jit(solution)/shard_map/ppermute | solution.py:24
  251.4 105.7 %collective-permute-start.9 = (f32[4,4,256]{2,1,0:T(4,128)S(1)}, f32[4,4,256]{2,1,0:T(4,128)S(1)}, u32[]{:S(2)}, u32[]{:S(2)}) collective-permute-start(f32[4,4,256]{2,1,0:T(4,128)S(1)} %fusion.35), channel_id=1, source_target_pairs={{16,0},{32,16},{48,32},{64,48},{80,64},{96,80},{112,96},{128,112},... | collective-permute-start | bytes 49160 | tf_op jit(solution)/shard_map/ppermute | solution.py:26
  358.2 5.0 %collective-permute-start.10 = (f32[4,1,512]{2,1,0:T(1,128)S(1)}, f32[4,1,512]{2,1,0:T(1,128)S(1)}, u32[]{:S(2)}, u32[]{:S(2)}) collective-permute-start(f32[4,1,512]{2,1,0:T(1,128)S(1)} %get-tuple-element.117), channel_id=1, source_target_pairs={{1,0},{2,1},{3,2},{4,3},{5,4},{6,5},{7,6},{8,7},{9,8},{10,9},{11,1... | collective-permute-start | bytes 24584 | tf_op jit(solution)/shard_map/ppermute | solution.py:26
  360.1 6.2 %collective-permute-start.11 = (f32[4,1,512]{2,1,0:T(1,128)S(1)}, f32[4,1,512]{2,1,0:T(1,128)S(1)}, u32[]{:S(2)}, u32[]{:S(2)}) collective-permute-start(f32[4,1,512]{2,1,0:T(1,128)S(1)} %get-tuple-element.118), channel_id=1, source_target_pairs={{0,1},{1,2},{2,3},{3,4},{4,5},{5,6},{6,7},{7,8},{8,9},{9,10},{10,1... | collective-permute-start | bytes 24584 | tf_op jit(solution)/shard_map/ppermute | solution.py:24
  367.3 14.2 %collective-permute-start.12 = (f32[4,4,256]{2,1,0:T(4,128)S(1)}, f32[4,4,256]{2,1,0:T(4,128)S(1)}, u32[]{:S(2)}, u32[]{:S(2)}) collective-permute-start(f32[4,4,256]{2,1,0:T(4,128)S(1)} %fusion.33), channel_id=1, source_target_pairs={{0,16},{16,32},{32,48},{48,64},{64,80},{80,96},{96,112},{112,128},... | collective-permute-start | bytes 49160 | tf_op jit(solution)/shard_map/ppermute | solution.py:24
  379.5 9.0 %collective-permute-start.13 = (f32[4,4,256]{2,1,0:T(4,128)S(1)}, f32[4,4,256]{2,1,0:T(4,128)S(1)}, u32[]{:S(2)}, u32[]{:S(2)}) collective-permute-start(f32[4,4,256]{2,1,0:T(4,128)S(1)} %fusion.33), channel_id=1, source_target_pairs={{16,0},{32,16},{48,32},{64,48},{80,64},{96,80},{112,96},{128,112},... | collective-permute-start | bytes 49160 | tf_op jit(solution)/shard_map/ppermute | solution.py:26
where the time goes:
time: 393 us; the launch traced here: 390 us
  starting transfers between devices  150 us (38%)
  other arithmetic  93.6 us (24%)
  local copies, waits for them, and re-layouts  56.8 us (14%)
  blocking collectives  32.4 us (8%)
  matrix products  29.9 us (8%)
  waiting for transfers between devices  21.2 us (5%)
  loops' own time  5.2 us (1%)
    ppermute x7, starting transfers between devices, padded_2(): lax.ppermute(head, axis, [((i + 1) % count, i) for i in range(ends)])  116 us
    ppermute x7, starting transfers between devices, padded_2(): lax.ppermute(tail, axis, [(i, (i + 1) % count) for i in range(ends)])  34.1 us
    select_n x1, other arithmetic, edge_tables(): jnp.where(col_of == 0, left_source, jnp.where(col_of == 3, right_source,...  31.2 us
    select_n x1, other arithmetic, edge_tables(): jnp.where(row_of == 0, lower_source, jnp.where(row_of == 3, upper_source,...  30.8 us
    dot_general x6, matrix products, one_step(): jnp.einsum('gf,nfc->ngc', coupling, current, precision=highest)  19 us
    all_gather x1, blocking collectives, shards(): every_change = lax.all_gather(change, 'lev', axis=0, tiled=True)  17.1 us
    all_gather x1, blocking collectives, shards(): every_host = lax.all_gather(host_columns, 'lev', axis=2, tiled=True)  15.3 us
    ppermute x7, waiting for transfers between devices, padded_2(): lax.ppermute(head, axis, [((i + 1) % count, i) for i in range(ends)])  15 us
  transfers between devices with their start and end apart: 14, of which 5 were waited for; matrix products, arithmetic and copies ran while one was open for 44% of the time, Pallas kernels for 0%

commit v1 on v0

--- a/solution.py
+++ b/solution.py
@@ -3,6 +3,7 @@
 import numpy as np
 from jax import lax
 from jax.sharding import PartitionSpec as P
+from jax.lax import all_to_all, axis_size
 
 CRM_X = 64
 lateral_mix = 0.2
@@ -156,7 +157,9 @@
     change = (
         (cloud_new - cloud_state).reshape(own_rows, n_fields, n_levels, cell_width).mean(axis=3)
     )
-    every_change = lax.all_gather(change, "lev", axis=0, tiled=True)
+    every_change = jnp.concatenate(
+        all_to_all(jnp.stack([change] * axis_size("lev")), "lev", 0, 0), axis=0
+    )
     level_change = lax.dynamic_slice_in_dim(every_change, lev_at * lev_dev, lev_dev, 2)
     column_tendency = jnp.einsum("vf,nfl->vln", feedback_map, level_change, precision=highest)
     physics = jnp.dot(

time: 393 us -> 378 us (0.962)
  blocking collectives: 32.4 us -> 15.1 us
  local copies, waits for them, and re-layouts: 56.8 us -> 48.4 us
  starting transfers between devices: 150 us -> 158 us
    all_gather x1 -> x0, blocking collectives: 17.1 us -> none  [shards(): every_change = lax.all_gather(change, 'lev', axis=0, tiled=True)]
    all_to_all x0 -> x1, starting transfers between devices: none -> 7.22 us  [shards(): all_to_all(jnp.stack([change] * axis_size('lev')), 'lev', 0, 0)]
    gather x4, local copies, waits for them, and re-layouts: 8.41 us -> 2.9 us  [edge_tables(): lower_ids = element_links[:, 2][elem_of] % elem_dev]
  transfers between devices with their start and end apart: 14 -> 15, of which waited for: 5 -> 5; matrix products, arithmetic and copies ran while one was open for 44% -> 44% of each run, Pallas kernels for 0% -> 0%
where the time goes in v1:
time: 378 us; the launch traced here: 375 us
  starting transfers between devices  158 us (42%)
  other arithmetic  95.3 us (25%)
  local copies, waits for them, and re-layouts  48.4 us (13%)
  matrix products  29.9 us (8%)
  waiting for transfers between devices  21.7 us (6%)
  blocking collectives  15.1 us (4%)
  loops' own time  5.2 us (1%)
    ppermute x7, starting transfers between devices, padded_2(): lax.ppermute(head, axis, [((i + 1) % count, i) for i in range(ends)])  118 us
    ppermute x7, starting transfers between devices, padded_2(): lax.ppermute(tail, axis, [(i, (i + 1) % count) for i in range(ends)])  33.2 us
    select_n x1, other arithmetic, edge_tables(): jnp.where(col_of == 0, left_source, jnp.where(col_of == 3, right_source,...  31.2 us
    select_n x1, other arithmetic, edge_tables(): jnp.where(row_of == 0, lower_source, jnp.where(row_of == 3, upper_source,...  31.1 us
    dot_general x6, matrix products, one_step(): jnp.einsum('gf,nfc->ngc', coupling, current, precision=highest)  19 us
    all_gather x1, blocking collectives, shards(): every_host = lax.all_gather(host_columns, 'lev', axis=2, tiled=True)  15.1 us
    ppermute x7, waiting for transfers between devices, padded_2(): lax.ppermute(head, axis, [((i + 1) % count, i) for i in range(ends)])  15 us
    add x6, local copies, waits for them, and re-layouts, one_step(): eastward + westward - 2.0 * current  9.86 us
  transfers between devices with their start and end apart: 15, of which 5 were waited for; matrix products, arithmetic and copies ran while one was open for 44% of the time, Pallas kernels for 0%

profile of v1, /device:TPU:230, one launch (start us, length us, event | category | flops | bytes accessed | tf_op | source)
XLA Modules:
  0.0 375.3 jit_solution(9304141950277809093)
XLA Ops:
  0.7 1.0 convolution_bitcast_fusion.4
  1.7 5.4 %collective-permute-start.4 = (f32[1,1,256]{2,1,0:T(1,128)S(1)}, f32[1,1,256]{2,1,0:T(1,128)S(1)}, u32[]{:S(2)}, u32[]{:S(2)}) collective-permute-start(f32[1,1,256]{2,1,0:T(1,128)S(1)} %convolution_bitcast_fusion.4), channel_id=1, source_target_pairs={{0,16},{16,32},{32,48},{48,64},{64,80},{80,96},{96,112},{112,128},... | collective-permute-start | bytes 3080 | tf_op jit(solution)/shard_map/ppermute | solution.py:25
  7.1 1.9 collective-permute-start.5
  10.2 15.1 %all_gather.3 = f32[128,4,64]{0,1,2:T(4,128)S(1)} all-gather(f32[128,4,4]{0,1,2:T(4,128)S(1)} %bitcast.240), channel_id=1, replica_groups=mesh['elem'=32,'lev'=16] {'lev'}, dimensions={2}, use_global_device_ids=true | all-gather | bytes 139264 | tf_op jit(solution)/shard_map/all_gather | solution.py:151
  25.6 1.5 fusion.127
  27.3 68.8 %while.13 = (s32[]{:T(128)}, f32[8,8,4096]{2,1,0:T(8,128)S(1)}, s32[]{:T(128)}, s32[8]{0:T(128)S(1)}, f32[8,8]{1,0:T(8,128)S(1)}, /*index=5*/f32[8,8,64]{2,1,0:T(8,128)S(1)}, s32[]{:T(128)}) while((s32[]{:T(128)}, f32[8,8,4096]{2,1,0:T(8,128)S(1)}, s32[]{:T(128)}, s32[8]{0:T(128)S(1)}, f32[8,8]{1,0:T(8,128)S(1)}, ...), condition=%wide.region_2.3_spmd.clone, body=%wide.region_1.2_spmd.clone.sunk | while | flops 28835848 | bytes 22041208 | solution.py:77
  28.1 0.8 reshape.1006
  30.4 1.2 maximum_add_fusion.2
  31.6 1.6 add.881
  33.8 1.6 reshape.1005
  35.5 3.2 fusion.176
  39.4 0.8 reshape.1006
  41.8 1.2 maximum_add_fusion.2
  42.9 1.6 add.881
  45.2 1.6 reshape.1005
  46.8 3.2 fusion.176
  53.1 1.2 maximum_add_fusion.2
  54.3 1.6 add.881
  56.5 1.6 reshape.1005
  58.1 3.2 fusion.176
  62.1 0.8 reshape.1006
  64.4 1.2 maximum_add_fusion.2
  65.6 1.6 add.881
  67.9 1.6 reshape.1005
  69.5 3.2 fusion.176
  73.4 0.8 reshape.1006
  75.8 1.2 maximum_add_fusion.2
  76.9 1.6 add.881
  79.2 1.6 reshape.1005
  80.8 3.2 fusion.176
  84.8 0.8 reshape.1006
  87.1 1.2 maximum_add_fusion.2
  88.3 1.6 add.881
  90.5 1.6 reshape.1005
  92.2 3.2 fusion.176
  96.1 1.8 sub.95
  97.9 2.2 reshape.408
  100.1 2.3 reduce_sum.9
  102.4 1.0 reshape.1001
  103.5 7.2 %all-to-all-start = ((f32[16,1,4096]{2,1,0:T(1,128)}), f32[16,1,4096]{2,1,0:T(1,128)S(1)}, u32[]{:S(2)}, u32[]{:S(2)}) async-start(f32[16,1,4096]{2,1,0:T(1,128)} %reshape.1001), calls=%async_computation | async-start | bytes 524288 | tf_op jit(solution)/shard_map/all_to_all | solution.py:161
  110.7 2.2 collective-permute-start
  112.9 2.3 collective-permute-start.1
  122.0 4.4 %select_select_fusion.3 = s32[512,1]{0,1:T(1,128)S(1)} fusion(s32[]{:T(128)} %bitcast.41, s32[]{:T(128)} %bitcast.42, s32[]{:T(128)} %bitcast.43, s32[]{:T(128)} %bitcast.44, s32[]{:T(128)} %bitcast.45, s32[]{:T(128)} %bitcast.47, s32[]{:T(128)} %bitcast.46), kind=kLoop, calls=%fused_computation.216 | loop fusion | flops 11776 | bytes 2076 | tf_op jit(solution)/shard_map/gather | solution.py:92
  126.4 4.5 %select_select_fusion.1 = s32[512,1]{0,1:T(1,128)S(1)} fusion(s32[]{:T(128)} %bitcast.107, s32[]{:T(128)} %bitcast.108, s32[]{:T(128)} %bitcast.109, s32[]{:T(128)} %bitcast.110, s32[]{:T(128)} %bitcast.111, s32[]{:T(128)} %bitcast.113, s32[]{:T(128)} %bitcast.112), kind=kLoop, calls=%fused_computation.214 | loop fusion | flops 11776 | bytes 2076 | tf_op jit(solution)/shard_map/gather | solution.py:102
  130.9 4.4 %select_select_fusion = s32[512,1]{0,1:T(1,128)S(1)} fusion(s32[]{:T(128)} %bitcast.140, s32[]{:T(128)} %bitcast.141, s32[]{:T(128)} %bitcast.142, s32[]{:T(128)} %bitcast.143, s32[]{:T(128)} %bitcast.144, s32[]{:T(128)} %bitcast.146, s32[]{:T(128)} %bitcast.145), kind=kLoop, calls=%fused_computation.213 | loop fusion | flops 11776 | bytes 2076 | tf_op jit(solution)/shard_map/gather | solution.py:103
  135.3 31.1 %fusion.104 = s32[512]{0:T(512)S(1)} fusion(pred[512]{0:T(512)(128)(4,1)S(1)} %compare_reduce_fusion, pred[512]{0:T(512)(128)(4,1)S(1)} %compare_reduce_fusion.1, pred[512]{0:T(512)(128)(4,1)S(1)} %compare_reduce_fusion.2, pred[512]{0:T(512)(128)(4,1)S(1)} %compare_reduce_fusion.3, pred[512]{0:T(512)(128)(4,1)S(1)} %compare_reduce_fusion.4, ...), kind=kLoop, calls=%fused_computation.204 | loop fusion | flops 53248 | bytes 19144 | tf_op jit(solution)/shard_map/jit(_where)/select_n | solution.py:106
  166.4 4.4 %select_select_fusion.2 = s32[512,1]{0,1:T(1,128)S(1)} fusion(s32[]{:T(128)} %bitcast.74, s32[]{:T(128)} %bitcast.75, s32[]{:T(128)} %bitcast.76, s32[]{:T(128)} %bitcast.77, s32[]{:T(128)} %bitcast.78, s32[]{:T(128)} %bitcast.80, s32[]{:T(128)} %bitcast.79), kind=kLoop, calls=%fused_computation.215 | loop fusion | flops 11776 | bytes 2076 | tf_op jit(solution)/shard_map/gather | solution.py:93
  170.8 31.2 %fusion.94 = s32[512]{0:T(512)S(1)} fusion(pred[512]{0:T(512)(128)(4,1)S(1)} %compare_reduce_fusion, pred[512]{0:T(512)(128)(4,1)S(1)} %compare_reduce_fusion.1, pred[512]{0:T(512)(128)(4,1)S(1)} %compare_reduce_fusion.2, pred[512]{0:T(512)(128)(4,1)S(1)} %compare_reduce_fusion.3, pred[512]{0:T(512)(128)(4,1)S(1)} %compare_reduce_fusion.4, ...), kind=kLoop, calls=%fused_computation.194 | loop fusion | flops 64512 | bytes 19148 | tf_op jit(solution)/shard_map/jit(_where)/select_n | solution.py:98
  203.1 1.3 reduce.50
  206.6 7.2 %collective-permute-start.2 = (f32[4,4,256]{2,1,0:T(4,128)S(1)}, f32[4,4,256]{2,1,0:T(4,128)S(1)}, u32[]{:S(2)}, u32[]{:S(2)}) collective-permute-start(f32[4,4,256]{2,1,0:T(4,128)S(1)} %fusion.37), channel_id=1, source_target_pairs={{0,16},{16,32},{32,48},{48,64},{64,80},{80,96},{96,112},{112,128},... | collective-permute-start | bytes 49160 | tf_op jit(solution)/shard_map/ppermute | solution.py:25
  213.9 1.9 collective-permute-start.3
  216.2 6.6 %collective-permute-done.3 = f32[4,4,256]{2,1,0:T(4,128)S(1)} collective-permute-done((f32[4,4,256]{2,1,0:T(4,128)S(1)}, f32[4,4,256]{2,1,0:T(4,128)S(1)}, u32[]{:S(2)}, u32[]{:S(2)}) %collective-permute-start.3) | collective-permute-done | bytes 16416 | tf_op jit(solution)/shard_map/ppermute | solution.py:27
  224.0 3.1 collective-permute-start.6
  227.1 1.9 collective-permute-start.7
  229.7 3.6 collective-permute-done.7
  234.3 1.9 collective-permute-start.8
  236.2 104.8 %collective-permute-start.9 = (f32[4,4,256]{2,1,0:T(4,128)S(1)}, f32[4,4,256]{2,1,0:T(4,128)S(1)}, u32[]{:S(2)}, u32[]{:S(2)}) collective-permute-start(f32[4,4,256]{2,1,0:T(4,128)S(1)} %fusion.35), channel_id=1, source_target_pairs={{16,0},{32,16},{48,32},{64,48},{80,64},{96,80},{112,96},{128,112},... | collective-permute-start | bytes 49160 | tf_op jit(solution)/shard_map/ppermute | solution.py:27
  341.1 1.4 collective-permute-done.9
  343.6 1.9 collective-permute-start.10
  345.5 2.4 collective-permute-start.11
  348.6 3.1 collective-permute-done.11
  352.6 12.0 %collective-permute-start.12 = (f32[4,4,256]{2,1,0:T(4,128)S(1)}, f32[4,4,256]{2,1,0:T(4,128)S(1)}, u32[]{:S(2)}, u32[]{:S(2)}) collective-permute-start(f32[4,4,256]{2,1,0:T(4,128)S(1)} %fusion.33), channel_id=1, source_target_pairs={{0,16},{16,32},{32,48},{48,64},{64,80},{80,96},{96,112},{112,128},... | collective-permute-start | bytes 49160 | tf_op jit(solution)/shard_map/ppermute | solution.py:25
  364.6 1.9 collective-permute-start.13
  366.6 7.0 %collective-permute-done.13 = f32[4,4,256]{2,1,0:T(4,128)S(1)} collective-permute-done((f32[4,4,256]{2,1,0:T(4,128)S(1)}, f32[4,4,256]{2,1,0:T(4,128)S(1)}, u32[]{:S(2)}, u32[]{:S(2)}) %collective-permute-start.13) | collective-permute-done | bytes 16416 | tf_op jit(solution)/shard_map/ppermute | solution.py:27
  (151 shorter events, 32.9 us)
Async XLA Ops:
  0.6 26.4 %copy-start = (f32[8,4]{0,1:T(4,128)S(1)}, f32[8,4]{0,1:T(4,128)}, u32[]{:S(2)}) copy-start(f32[8,4]{0,1:T(4,128)} %param.20) | copy-start | bytes 388
  0.6 26.6 %copy-start.2 = (f32[8,8,4096]{2,1,0:T(8,128)S(1)}, f32[8,8,4096]{2,1,0:T(8,128)}, u32[]{:S(2)}) copy-start(f32[8,8,4096]{2,1,0:T(8,128)} %param.13) | copy-start | bytes 3145732
  0.7 26.6 %copy-start.7 = (f32[8,8]{1,0:T(8,128)S(1)}, f32[8,8]{1,0:T(8,128)}, u32[]{:S(2)}) copy-start(f32[8,8]{1,0:T(8,128)} %param.19) | copy-start | bytes 772
  1.7 200.3 %collective-permute-start.4 = (f32[1,1,256]{2,1,0:T(1,128)S(1)}, f32[1,1,256]{2,1,0:T(1,128)S(1)}, u32[]{:S(2)}, u32[]{:S(2)}) collective-permute-start(f32[1,1,256]{2,1,0:T(1,128)S(1)} %convolution_bitcast_fusion.4), channel_id=1, source_target_pairs={{0,16},{16,32},{32,48},{48,64},{64,80},{80,96},{96,112},{112,128},... | collective-permute-start | bytes 3080 | tf_op jit(solution)/shard_map/ppermute | solution.py:25
  7.1 194.9 %collective-permute-start.5 = (f32[1,1,256]{2,1,0:T(1,128)S(1)}, f32[1,1,256]{2,1,0:T(1,128)S(1)}, u32[]{:S(2)}, u32[]{:S(2)}) collective-permute-start(f32[1,1,256]{2,1,0:T(1,128)S(1)} %convolution_bitcast_fusion.4), channel_id=1, source_target_pairs={{16,0},{32,16},{48,32},{64,48},{80,64},{96,80},{112,96},{128,112},... | collective-permute-start | bytes 3080 | tf_op jit(solution)/shard_map/ppermute | solution.py:27
  96.0 4.0 %copy-start.1 = (f32[8,8,4096]{2,1,0:T(8,128)}, f32[8,8,4096]{2,1,0:T(8,128)S(1)}, u32[]{:S(2)}) copy-start(f32[8,8,4096]{2,1,0:T(8,128)S(1)} %get-tuple-element.80) | copy-start | bytes 3145732
  100.0 10.6 %copy-start.6 = (f32[4,4,512]{2,1,0:T(4,128)S(1)}, f32[4,4,512]{2,1,0:T(4,128)}, u32[]{:S(2)}) copy-start(f32[4,4,512]{2,1,0:T(4,128)} %param.16) | copy-start | bytes 98308
  100.0 15.2 %copy-start.5 = (s32[32,4]{0,1:T(4,128)S(1)}, s32[32,4]{0,1:T(4,128)}, u32[]{:S(2)}) copy-start(s32[32,4]{0,1:T(4,128)} %param.15) | copy-start | bytes 1540
  100.0 21.1 %copy-start.9 = (f32[2,4,512]{2,1,0:T(4,128)S(1)}, f32[2,4,512]{2,1,0:T(4,128)}, u32[]{:S(2)}) copy-start(f32[2,4,512]{2,1,0:T(4,128)} %param.17) | copy-start | bytes 49156
  100.1 21.2 %copy-start.4 = (f32[512,512,1]{1,0,2:T(8,128)S(1)}, f32[512,512,1]{1,0,2:T(8,128)}, u32[]{:S(2)}) copy-start(f32[512,512,1]{1,0,2:T(8,128)} %constant.378) | copy-start | bytes 3145732
  102.4 100.2 %copy-start.8 = (f32[512]{0:T(512)S(1)}, f32[512]{0:T(512)}, u32[]{:S(2)}) copy-start(f32[512]{0:T(512)} %param.18) | copy-start | bytes 6148
  103.5 99.2 %all-to-all-start = ((f32[16,1,4096]{2,1,0:T(1,128)}), f32[16,1,4096]{2,1,0:T(1,128)S(1)}, u32[]{:S(2)}, u32[]{:S(2)}) async-start(f32[16,1,4096]{2,1,0:T(1,128)} %reshape.1001), calls=%async_computation | async-start | bytes 524288 | tf_op jit(solution)/shard_map/all_to_all | solution.py:161
  110.7 94.8 %collective-permute-start = (f32[4,1,512]{2,1,0:T(1,128)S(1)}, f32[4,1,512]{2,1,0:T(1,128)S(1)}, u32[]{:S(2)}, u32[]{:S(2)}) collective-permute-start(f32[4,1,512]{2,1,0:T(1,128)S(1)} %get-tuple-element.121), channel_id=1, source_target_pairs={{1,0},{2,1},{3,2},{4,3},{5,4},{6,5},{7,6},{8,7},{9,8},{10,9},{11,1... | collective-permute-start | bytes 24584 | tf_op jit(solution)/shard_map/ppermute | solution.py:27
  112.9 92.7 %collective-permute-start.1 = (f32[4,1,512]{2,1,0:T(1,128)S(1)}, f32[4,1,512]{2,1,0:T(1,128)S(1)}, u32[]{:S(2)}, u32[]{:S(2)}) collective-permute-start(f32[4,1,512]{2,1,0:T(1,128)S(1)} %get-tuple-element.122), channel_id=1, source_target_pairs={{0,1},{1,2},{2,3},{3,4},{4,5},{5,6},{6,7},{7,8},{8,9},{9,10},{10,1... | collective-permute-start | bytes 24584 | tf_op jit(solution)/shard_map/ppermute | solution.py:25
  122.0 83.1 %copy-start.10 = (f32[4,8]{1,0:T(4,128)S(1)}, f32[4,8]{1,0:T(4,128)}, u32[]{:S(2)}) copy-start(f32[4,8]{1,0:T(4,128)} %param.21) | copy-start | bytes 388
  122.0 83.6 %copy-start.3 = (f32[512,512,1]{1,0,2:T(8,128)S(1)}, f32[512,512,1]{1,0,2:T(8,128)}, u32[]{:S(2)}) copy-start(f32[512,512,1]{1,0,2:T(8,128)} %constant.379) | copy-start | bytes 3145732
  206.6 9.6 %collective-permute-start.2 = (f32[4,4,256]{2,1,0:T(4,128)S(1)}, f32[4,4,256]{2,1,0:T(4,128)S(1)}, u32[]{:S(2)}, u32[]{:S(2)}) collective-permute-start(f32[4,4,256]{2,1,0:T(4,128)S(1)} %fusion.37), channel_id=1, source_target_pairs={{0,16},{16,32},{32,48},{48,64},{64,80},{80,96},{96,112},{112,128},... | collective-permute-start | bytes 49160 | tf_op jit(solution)/shard_map/ppermute | solution.py:25
  213.9 9.0 %collective-permute-start.3 = (f32[4,4,256]{2,1,0:T(4,128)S(1)}, f32[4,4,256]{2,1,0:T(4,128)S(1)}, u32[]{:S(2)}, u32[]{:S(2)}) collective-permute-start(f32[4,4,256]{2,1,0:T(4,128)S(1)} %fusion.37), channel_id=1, source_target_pairs={{16,0},{32,16},{48,32},{64,48},{80,64},{96,80},{112,96},{128,112},... | collective-permute-start | bytes 49160 | tf_op jit(solution)/shard_map/ppermute | solution.py:27
  224.0 5.7 %collective-permute-start.6 = (f32[4,1,512]{2,1,0:T(1,128)S(1)}, f32[4,1,512]{2,1,0:T(1,128)S(1)}, u32[]{:S(2)}, u32[]{:S(2)}) collective-permute-start(f32[4,1,512]{2,1,0:T(1,128)S(1)} %get-tuple-element.119), channel_id=1, source_target_pairs={{1,0},{2,1},{3,2},{4,3},{5,4},{6,5},{7,6},{8,7},{9,8},{10,9},{11,1... | collective-permute-start | bytes 24584 | tf_op jit(solution)/shard_map/ppermute | solution.py:27
  227.1 6.2 %collective-permute-start.7 = (f32[4,1,512]{2,1,0:T(1,128)S(1)}, f32[4,1,512]{2,1,0:T(1,128)S(1)}, u32[]{:S(2)}, u32[]{:S(2)}) collective-permute-start(f32[4,1,512]{2,1,0:T(1,128)S(1)} %get-tuple-element.120), channel_id=1, source_target_pairs={{0,1},{1,2},{2,3},{3,4},{4,5},{5,6},{6,7},{7,8},{8,9},{9,10},{10,1... | collective-permute-start | bytes 24584 | tf_op jit(solution)/shard_map/ppermute | solution.py:25
  234.3 106.8 %collective-permute-start.8 = (f32[4,4,256]{2,1,0:T(4,128)S(1)}, f32[4,4,256]{2,1,0:T(4,128)S(1)}, u32[]{:S(2)}, u32[]{:S(2)}) collective-permute-start(f32[4,4,256]{2,1,0:T(4,128)S(1)} %fusion.35), channel_id=1, source_target_pairs={{0,16},{16,32},{32,48},{48,64},{64,80},{80,96},{96,112},{112,128},... | collective-permute-start | bytes 49160 | tf_op jit(solution)/shard_map/ppermute | solution.py:25
  236.2 106.3 %collective-permute-start.9 = (f32[4,4,256]{2,1,0:T(4,128)S(1)}, f32[4,4,256]{2,1,0:T(4,128)S(1)}, u32[]{:S(2)}, u32[]{:S(2)}) collective-permute-start(f32[4,4,256]{2,1,0:T(4,128)S(1)} %fusion.35), channel_id=1, source_target_pairs={{16,0},{32,16},{48,32},{64,48},{80,64},{96,80},{112,96},{128,112},... | collective-permute-start | bytes 49160 | tf_op jit(solution)/shard_map/ppermute | solution.py:27
  343.6 5.0 %collective-permute-start.10 = (f32[4,1,512]{2,1,0:T(1,128)S(1)}, f32[4,1,512]{2,1,0:T(1,128)S(1)}, u32[]{:S(2)}, u32[]{:S(2)}) collective-permute-start(f32[4,1,512]{2,1,0:T(1,128)S(1)} %get-tuple-element.117), channel_id=1, source_target_pairs={{1,0},{2,1},{3,2},{4,3},{5,4},{6,5},{7,6},{8,7},{9,8},{10,9},{11,1... | collective-permute-start | bytes 24584 | tf_op jit(solution)/shard_map/ppermute | solution.py:27
  345.5 6.2 %collective-permute-start.11 = (f32[4,1,512]{2,1,0:T(1,128)S(1)}, f32[4,1,512]{2,1,0:T(1,128)S(1)}, u32[]{:S(2)}, u32[]{:S(2)}) collective-permute-start(f32[4,1,512]{2,1,0:T(1,128)S(1)} %get-tuple-element.118), channel_id=1, source_target_pairs={{0,1},{1,2},{2,3},{3,4},{4,5},{5,6},{6,7},{7,8},{8,9},{9,10},{10,1... | collective-permute-start | bytes 24584 | tf_op jit(solution)/shard_map/ppermute | solution.py:25
  352.6 13.9 %collective-permute-start.12 = (f32[4,4,256]{2,1,0:T(4,128)S(1)}, f32[4,4,256]{2,1,0:T(4,128)S(1)}, u32[]{:S(2)}, u32[]{:S(2)}) collective-permute-start(f32[4,4,256]{2,1,0:T(4,128)S(1)} %fusion.33), channel_id=1, source_target_pairs={{0,16},{16,32},{32,48},{48,64},{64,80},{80,96},{96,112},{112,128},... | collective-permute-start | bytes 49160 | tf_op jit(solution)/shard_map/ppermute | solution.py:25
  364.6 9.0 %collective-permute-start.13 = (f32[4,4,256]{2,1,0:T(4,128)S(1)}, f32[4,4,256]{2,1,0:T(4,128)S(1)}, u32[]{:S(2)}, u32[]{:S(2)}) collective-permute-start(f32[4,4,256]{2,1,0:T(4,128)S(1)} %fusion.33), channel_id=1, source_target_pairs={{16,0},{32,16},{48,32},{64,48},{80,64},{96,80},{112,96},{128,112},... | collective-permute-start | bytes 49160 | tf_op jit(solution)/shard_map/ppermute | solution.py:27
